TPU v7x, 32 devices: a whole 2x2x4 slice. The times are simulated.
32 devices in a mesh: dp: 2 (over x), tp: 4 (over z), ep: 4 (over y, core).
Axes of the slice: x: 2, y: 2, z: 4, core: 2. Of those that a mesh axis runs over, the one named last changes fastest.
Arguments:
- tokens_x: bfloat16 [2048, 2048], P(('dp', 'ep', 'tp')), parts along dimension 0
- expert_ids: int32 [2048, 6], P(('dp', 'ep', 'tp')), parts along dimension 0
- route_gate: float32 [2048, 6], P(('dp', 'ep', 'tp')), parts along dimension 0
- w_gate: bfloat16 [64, 2048, 1408], P('ep', None, 'tp')
- w_up: bfloat16 [64, 2048, 1408], P('ep', None, 'tp')
- w_down: bfloat16 [64, 1408, 2048], P('ep', 'tp')
Outputs:
- output: bfloat16 [2048, 2048], P(('dp', 'ep', 'tp')), parts along dimension 0
There are 2 independent parts. A program takes and returns all parts, laid end to end along the dimension named above; an argument that names none is the same for every part.
All inputs are finite; a program needn't handle non-finite values.
Results may differ from a plain program's by a relative error of at most 0.00123.
Values are sent between devices in bfloat16 or wider.
A program may use at most 1 GiB of HBM per device.

v0:
```python
import jax
import jax.numpy as jnp
from jax import lax
from jax.sharding import PartitionSpec as P, NamedSharding


def solution(mesh):
    ep_size = mesh.shape['ep']
    row_spec = P(('dp', 'ep', 'tp'), None)
    w_in_spec = P('ep', None, 'tp')
    w_out_spec = P('ep', 'tp', None)

    def local_moe(x_local, ids_local, gate_local, w_gate, w_up, w_down):
        e_local = w_gate.shape[0]
        x_all = lax.all_gather(x_local, ('ep', 'tp'), tiled=True)
        ids_all = lax.all_gather(ids_local, ('ep', 'tp'), tiled=True)
        gate_all = lax.all_gather(gate_local, ('ep', 'tp'), tiled=True)
        num_tok, top_k = ids_all.shape
        local_pairs = num_tok * top_k // ep_size
        expert_cap = local_pairs // e_local
        local_ids = ids_all.reshape(-1) - lax.axis_index('ep') * e_local
        is_local = (local_ids >= 0) & (local_ids < e_local)
        sort_order = jnp.argsort(jnp.where(is_local, local_ids, e_local), stable=True)[:local_pairs]
        tok_rows = sort_order // top_k
        gate_rows = gate_all.reshape(-1)[sort_order]
        x_rows = x_all[tok_rows].reshape(e_local, expert_cap, -1)
        h_gate = jnp.einsum('ecd,edf->ecf', x_rows, w_gate, preferred_element_type=jnp.float32)
        h_up = jnp.einsum('ecd,edf->ecf', x_rows, w_up, preferred_element_type=jnp.float32)
        hidden = (jax.nn.silu(h_gate) * h_up).astype(jnp.bfloat16)
        out_rows = jnp.einsum('ecf,efd->ecd', hidden, w_down, preferred_element_type=jnp.float32)
        out_rows = out_rows.reshape(local_pairs, -1) * gate_rows[:, None]
        partial_sum = jax.ops.segment_sum(out_rows, tok_rows, num_segments=num_tok)
        y_local = lax.psum_scatter(partial_sum, ('ep', 'tp'), scatter_dimension=0, tiled=True)
        return y_local.astype(jnp.bfloat16)

    return jax.shard_map(local_moe, mesh=mesh, in_specs=(row_spec, row_spec, row_spec, w_in_spec, w_in_spec, w_out_spec), out_specs=row_spec, check_vma=False)
```

profile of v0, /device:TPU:0, one launch (start us, length us, event | category | flops | bytes accessed | tf_op | source)
XLA Modules:
  0.0 285.3 jit_solution(11052183691264198378)
XLA Ops:
  6.5 0.0 all-gather.4.cloned.1.call-start
  6.5 0.7 all-gather.4.cloned.1.call-update
  7.3 0.0 reduce-scatter.2.cloned.1.call-start
  7.3 34.8 %all-gather.1 = f32[16,64,6]{1,2,0:T(8,128)S(1)} all-gather(f32[1,64,6]{1,2,0:T(8,128)} %bitcast.12), channel_id=1, replica_groups=mesh['dp'=2,'tp'=4,'ep'=4] {'ep','tp'}, dimensions={0}, use_global_device_ids=true | all-gather | bytes 26112 | tf_op jit(solution)/shard_map/all_gather | solution.py:17
  42.1 0.2 copy.13
  42.4 0.3 reshape.15
  42.7 29.3 %all-gather = s32[16,64,6]{1,2,0:T(8,128)S(1)} all-gather(s32[1,64,6]{1,2,0:T(8,128)} %bitcast.13), channel_id=1, replica_groups=mesh['dp'=2,'tp'=4,'ep'=4] {'ep','tp'}, dimensions={0}, use_global_device_ids=true | all-gather | bytes 26112 | tf_op jit(solution)/shard_map/all_gather | solution.py:16
  72.0 0.2 copy.12
  72.2 0.3 sub.17
  72.6 6.7 %sort.17 = (s32[6144]{0:T(1024)}, s32[6144]{0:T(1024)S(1)}) sort(s32[6144]{0:T(1024)S(1)} %and_select_fusion, s32[6144]{0:T(1024)S(1)} %iota.4), dimensions={0}, to_apply=%region_0.1 | sort | flops 79872 | bytes 98304 | tf_op jit(solution)/shard_map/jit(argsort)/sort | solution.py:23
  79.4 8.6 %gather_fusion.1 = f32[1536]{0:T(1024)S(1)} fusion(f32[6144]{0:T(1024)S(1)} %reshape.15, s32[2048]{0:T(1024)S(1)} %pad_clamp_fusion), kind=kCustom, calls=%fused_computation.1 | custom fusion | bytes 18432 | tf_op jit(solution)/shard_map/gather | solution.py:25
  88.0 0.0 all-gather.4.cloned.1.call-done
  88.0 15.5 %gather_fusion = bf16[1536,2048]{1,0:T(8,128)(2,1)} fusion(bf16[1024,2048]{1,0:T(8,128)(2,1)} %all-gather.4.cloned.1.call-done, s32[2048]{0:T(1024)S(1)} %pad_clamp_fusion.1), kind=kCustom, calls=%fused_computation | custom fusion | bytes 12589056 | tf_op jit(solution)/shard_map/gather | solution.py:26
  103.5 12.9 %fusion.6 = f32[16,96,352]{2,1,0:T(8,128)S(1)} fusion(bf16[16,96,2048]{2,1,0:T(8,128)(2,1)} %bitcast.10, bf16[16,2048,352]{1,2,0:T(8,128)(2,1)} %param.9), kind=kOutput, calls=%fused_computation.20 | convolution fusion | flops 2214592512 | bytes 31522816 | tf_op jit(solution)/shard_map/ecd,edf->ecf/dot_general | solution.py:27
  116.3 23.2 %fusion.2 = f32[16,96,2048]{2,1,0:T(8,128)} fusion(bf16[16,352,2048]{2,1,0:T(8,128)(2,1)} %param.11, f32[16,96,352]{2,1,0:T(8,128)S(1)} %fusion.6, bf16[16,96,2048]{2,1,0:T(8,128)(2,1)} %bitcast.11, bf16[16,2048,352]{1,2,0:T(8,128)(2,1)} %param.10), kind=kOutput, calls=%fused_computation.7 | convolution fusion | flops 4432429056 | bytes 67174400 | tf_op jit(solution)/shard_map/ecf,efd->ecd/dot_general | solution.py:30
  139.6 9.9 %bitcast_multiply_fusion = f32[1536,2048]{1,0:T(8,128)} fusion(f32[16,96,2048]{2,1,0:T(8,128)} %fusion.2, f32[1536]{0:T(1024)S(1)} %gather_fusion.1), kind=kLoop, calls=%fused_computation.3 | loop fusion | flops 3145728 | bytes 25171968 | tf_op jit(solution)/shard_map/mul | solution.py:31
  149.5 24.8 %scatter_custom_fusion = f32[1024,2048]{1,0:T(8,128)} fusion(s32[1536]{0:T(1024)S(1)} %get-tuple-element.8, f32[1536,2048]{1,0:T(8,128)} %bitcast_multiply_fusion, f32[]{:T(128)} %constant.10.clone.1), kind=kCustom, calls=%fused_computation.4 | custom fusion | flops 3145728 | bytes 8389120 | tf_op jit(solution)/shard_map/scatter-add | solution.py:32
  174.3 0.0 reduce-scatter.2.cloned.1.call-update
  174.4 102.4 %reduce-scatter.2.cloned.1.call-done = f32[64,2048]{1,0:T(8,128)} async-done(((f32[1024,2048]{1,0:T(8,128)}), f32[64,2048]{1,0:T(8,128)}) %reduce-scatter.2.cloned.1.call-update) | async-done | bytes 524304 | tf_op jit(solution)/shard_map/reduce_scatter | solution.py:33
  276.7 1.8 convert_element_type.7
  (6 shorter events, 0.1 us)
Async XLA Ops:
  6.5 81.5 %all-gather.4.cloned.1.call-start = ((), (), s32[]{:S(2)}) async-start(), calls=%async_computation.1 | async-start | bytes 4456448 | tf_op jit(solution)/shard_map/all_gather | solution.py:15
  7.3 269.5 %reduce-scatter.2.cloned.1.call-start = ((), (), s32[]{:S(2)}) async-start(), calls=%async_computation.2 | async-start | bytes 8912896 | tf_op jit(solution)/shard_map/reduce_scatter | solution.py:33
Sparse Core Ops, SparseCore 0:
  9.5 53.5 all-gather.3
  174.5 102.1 reduce-scatter.1
where the time goes:
time: 286 us; the launch traced here: 285 us
  waiting for transfers between devices  103 us (36%)
  blocking collectives  64.1 us (22%)
  other arithmetic  43.3 us (15%)
  matrix products  36.1 us (13%)
  local copies, waits for them, and re-layouts  25.2 us (9%)
  between operations  13.5 us (5%)
    reduce_scatter x1, waiting for transfers between devices, local_moe(): lax.psum_scatter(partial_sum, ('ep', 'tp'), scatter_dimension=0, tiled=True)  102 us
    all_gather x1, blocking collectives, local_moe(): gate_all = lax.all_gather(gate_local, ('ep', 'tp'), tiled=True)  34.8 us
    all_gather x1, blocking collectives, local_moe(): ids_all = lax.all_gather(ids_local, ('ep', 'tp'), tiled=True)  29.3 us
    scatter-add x1, other arithmetic, local_moe(): partial_sum = jax.ops.segment_sum(out_rows, tok_rows, num_segments=num_tok)  24.8 us
    dot_general x1, matrix products, local_moe(): jnp.einsum('ecf,efd->ecd', hidden, w_down, preferred_element_type=jnp.flo...  23.2 us
    gather x1, local copies, waits for them, and re-layouts, local_moe(): x_rows = x_all[tok_rows].reshape(e_local, expert_cap, -1)  15.5 us
    dot_general x1, matrix products, local_moe(): jnp.einsum('ecd,edf->ecf', x_rows, w_gate, preferred_element_type=jnp.flo...  12.9 us
    mul x1, other arithmetic, local_moe(): out_rows = out_rows.reshape(local_pairs, -1) * gate_rows[:, None]  9.92 us
  transfers between devices with their start and end apart: 2, of which 1 were waited for; matrix products, arithmetic and copies ran while one was open for 6% of the time, Pallas kernels for 0%

commit v1 on v0

v1 whole, which is shorter than its diff:
```python
import functools

import jax
import jax.numpy as jnp
from jax import lax
from jax.experimental import pallas as pl
from jax.experimental.pallas import tpu as pltpu
from jax.sharding import PartitionSpec as P

MESH = pl.DeviceIdType.MESH
NK = 4
CW = 256
GRP = 4
SLOTS = 8
ROWS = 64
TOPK = 6


def moe_kernel(x_ref, ids_ref, gate_ref, wg, wu, wd, out_ref,
               xall, xg, meta, pmat, cmat, gbuf, acc_a, acc_b, hbuf, obuf,
               wgs, wus, wds, pown, psib, rd, rfar, rnear, ry,
               ags, agr, mss, msr, wsem, wdsem,
               ds_s, ds_r, fs_s, fs_r, ns_s, ns_r, ys_s, ys_r):
    f32, bf16 = jnp.float32, jnp.bfloat16
    d_model = x_ref.shape[1]
    kw = d_model // NK
    nc = d_model // CW
    n_exp = wg.shape[0]
    n_grp = n_exp // GRP

    z = lax.axis_index("tp")
    ep = lax.axis_index("ep")
    y = ep // 2
    c = ep % 2
    zn = (z + 1) % 4
    zq = (z + 3) % 4
    zo = (z + 2) % 4
    sib = {"ep": 2 * y + 1 - c}
    yn = {"ep": 2 * (1 - y) + c}
    zp = {"tp": zn}
    zm = {"tp": zq}
    sends = []

    def rcopy(src, dst, ssem, rsem, dev):
        return pltpu.make_async_remote_copy(src_ref=src, dst_ref=dst, send_sem=ssem, recv_sem=rsem,
                                            device_id=dev, device_id_type=MESH)

    def send(*args):
        copy = rcopy(*args)
        copy.start()
        sends.append(copy)

    def w_copies(k, g):
        rows = pl.ds(g * GRP, GRP)
        cols = pl.ds(k * kw, kw)
        return (pltpu.make_async_copy(wg.at[rows, cols, :], wgs.at[g], wsem.at[0, g]),
                pltpu.make_async_copy(wu.at[rows, cols, :], wus.at[g], wsem.at[1, g]))

    def wd_copy(n, g):
        rows = pl.ds(g * GRP, GRP)
        return pltpu.make_async_copy(wd.at[rows, :, pl.ds(n * CW, CW)], wds.at[n % 2, rows], wdsem.at[n % 2, g])

    for g in range(n_grp):
        for copy in w_copies(0, g):
            copy.start()
    for n in range(2):
        for g in range(n_grp):
            wd_copy(n, g).start()

    barrier = pltpu.get_barrier_semaphore()
    peers = [{"ep": (ep + d // 4) % 4, "tp": (z + d % 4) % 4} for d in range(1, 16)]
    for peer in peers:
        pl.semaphore_signal(barrier, inc=1, device_id=peer, device_id_type=MESH)
    pl.semaphore_wait(barrier, 15)

    def idx(cc, yy, zz):
        return cc * 8 + yy * 4 + zz

    me = idx(c, y, z)

    def send_block(k, slot, b, dev):
        src = x_ref.at[:, pl.ds(k * kw, kw)] if b is me else xall.at[k, b]
        send(src, xall.at[k, b], ags.at[k, slot], agr.at[k, b], dev)

    def wait_block(k, b):
        rcopy(xall.at[k, b], xall.at[k, b], ags.at[k, 0], agr.at[k, b], sib).wait_recv()

    y_own = idx(c, 1 - y, z)

    def step_f_own(k):
        send_block(k, 2, me, zp)
        send_block(k, 3, me, zm)
        send_block(k, 1, me, sib)

    def step_f_other(k):
        wait_block(k, y_own)
        send_block(k, 4, y_own, zp)
        send_block(k, 5, y_own, zm)
        send_block(k, 6, y_own, sib)

    def step_a(k):
        b = idx(c, y, zq)
        wait_block(k, b)
        send_block(k, 7, b, zp)
        send_block(k, 9, b, sib)
        b = idx(c, 1 - y, zn)
        wait_block(k, b)
        send_block(k, 8, b, zm)
        send_block(k, 10, b, sib)
        b = idx(c, y, zn)
        wait_block(k, b)
        send_block(k, 11, b, sib)
        b = idx(c, 1 - y, zq)
        wait_block(k, b)
        send_block(k, 12, b, sib)

    def step_b(k):
        b = idx(c, y, zo)
        wait_block(k, b)
        send_block(k, 13, b, sib)
        b = idx(c, 1 - y, zo)
        wait_block(k, b)
        send_block(k, 14, b, sib)

    def wait_sibling(k):
        for b in range(8):
            wait_block(k, (1 - c) * 8 + b)

    send_block(0, 0, me, yn)
    step_f_own(0)
    for k in range(1, NK):
        send_block(k, 0, me, yn)

    lane = lax.broadcasted_iota(jnp.int32, (128, 128), 1)
    sub = lax.broadcasted_iota(jnp.int32, (128, 128), 0)
    tri = jnp.where((sub < lane % ROWS) & (sub < ROWS), 1.0, 0.0).astype(bf16)

    def flip(v):
        v = jnp.concatenate([v, jnp.zeros((ROWS, 128 - TOPK), f32)], axis=1)
        v = jnp.concatenate([v, v], axis=0)
        return v.T[:8]

    ids_t = flip(ids_ref[...].astype(f32))
    gate_t = flip(gate_ref[...])
    exp_id = lax.broadcasted_iota(jnp.int32, (64, 128), 0).astype(f32)
    hits = [jnp.where(exp_id == ids_t[j:j + 1], 1.0, 0.0) for j in range(TOPK)]
    chosen = functools.reduce(lambda p, q: p + q, hits)
    rank = jnp.dot(chosen.astype(bf16), tri, preferred_element_type=f32)
    code = [SLOTS * ids_t[j:j + 1] + jnp.sum(rank * hits[j], axis=0, keepdims=True) for j in range(TOPK)]
    code = jnp.concatenate(code + [jnp.full((8 - TOPK, 128), -1.0, f32)], axis=0)
    meta[me, 0:8, :] = code
    meta[me, 8:16, :] = gate_t
    for k in range(NK):
        xall[k, me] = x_ref[:, k * kw:(k + 1) * kw]
    for d, peer in enumerate(peers):
        send(meta.at[me], meta.at[me], mss.at[d], msr.at[me], peer)

    step_f_other(0)
    step_a(0)
    if NK > 1:
        step_f_own(1)
        step_f_other(1)

    for d in range(1, 16):
        s_ep, s_z = (ep + d // 4) % 4, (z + d % 4) % 4
        b = idx(s_ep % 2, s_ep // 2, s_z)
        rcopy(meta.at[b], meta.at[b], mss.at[0], msr.at[b], sib).wait_recv()

    def build(p, carry):
        half = lax.broadcasted_iota(jnp.int32, (8, 128), 1) < ROWS
        both = jnp.where(half, meta[2 * p, 0:8, :], meta[2 * p + 1, 0:8, :]).astype(jnp.int32)
        gts = jnp.where(half, meta[2 * p, 8:16, :], meta[2 * p + 1, 8:16, :])
        expert = lax.shift_right_arithmetic(both, 3)
        slot = both - expert * SLOTS
        row = (expert - ep * n_exp) * (2 * SLOTS) + jnp.where(half, 0, SLOTS) + slot
        r = lax.broadcasted_iota(jnp.int32, (n_exp * 2 * SLOTS, 128), 0)
        sel = jnp.zeros(r.shape, f32)
        wts = jnp.zeros(r.shape, f32)
        for j in range(TOPK):
            eq = r == row[j:j + 1]
            sel = jnp.where(eq, 1.0, sel)
            wts = jnp.where(eq, gts[j:j + 1], wts)
        pmat[p] = sel.astype(bf16)
        selt = sel.T.astype(bf16)
        cmat[p] = jnp.concatenate([selt, selt, selt], axis=1)
        per_row = jnp.broadcast_to(jnp.sum(wts, axis=1, keepdims=True), wts.shape)
        for e in range(n_exp):
            gbuf[e, pl.ds(p * 16, 16), :] = per_row[e * 16:(e + 1) * 16]
        return carry

    lax.fori_loop(0, 8, build, 0)
    step_b(0)

    def compute(k):
        def gather(i, carry):
            for u in range(2):
                p = i * 2 + u
                rows = xall[k, pl.ds(2 * p, 2)].reshape(2 * ROWS, kw)
                v = jnp.dot(pmat[p], rows, preferred_element_type=f32).astype(bf16)
                for e in range(n_exp):
                    xg[e, pl.ds(p * 16, 16), :] = v[e * 16:(e + 1) * 16]
            return carry

        lax.fori_loop(0, 4, gather, 0)

        def experts(g, carry):
            for copy in w_copies(k, g):
                copy.wait()
            for u in range(GRP):
                e = g * GRP + u
                xe = xg[e]
                a = jnp.dot(xe, wgs[g, u], preferred_element_type=f32)
                b = jnp.dot(xe, wus[g, u], preferred_element_type=f32)
                if k > 0:
                    a = acc_a[e] + a
                    b = acc_b[e] + b
                if k < NK - 1:
                    acc_a[e] = a
                    acc_b[e] = b
                else:
                    hbuf[e] = (jax.nn.silu(a) * b).astype(bf16)
            if k < NK - 1:
                for copy in w_copies(k + 1, g):
                    copy.start()
            return carry

        lax.fori_loop(0, n_grp, experts, 0)

    for k in range(NK):
        if k + 1 < NK:
            step_a(k + 1)
        if k + 2 < NK:
            step_f_own(k + 2)
            step_f_other(k + 2)
        wait_sibling(k)
        compute(k)
        if k + 1 < NK:
            step_b(k + 1)

    def down(n):
        def body(g, carry):
            wd_copy(n, g).wait()
            for u in range(GRP):
                e = g * GRP + u
                o = jnp.dot(hbuf[e], wds[n % 2, e], preferred_element_type=f32)
                gt = gbuf[e]
                o = o * jnp.concatenate([gt] * (CW // 128), axis=1)
                parts = []
                for i in range(3):
                    part = o.astype(bf16)
                    if i < 2:
                        o = o - part.astype(f32)
                    parts.append(part)
                for p in range(8):
                    for i in range(3):
                        obuf[pl.ds(p * 768 + i * 256 + e * 16, 16), :] = parts[i][p * 16:(p + 1) * 16]
            return carry

        lax.fori_loop(0, n_grp, body, 0)
        if n + 2 < nc:
            for g in range(n_grp):
                wd_copy(n + 2, g).start()

    def merged(p):
        v = jnp.dot(cmat[p], obuf[pl.ds(p * 768, 768), :], preferred_element_type=f32)
        return v.reshape(2, ROWS, CW)

    sib_sends = {}

    def combine(n):
        if n >= 2:
            for copy in sib_sends.pop(n - 2):
                copy.wait_send()
        out = []
        for q in range(4):
            psib[n % 2, 2 * q:2 * q + 2] = merged((1 - c) * 4 + q)
        for q in range(4):
            copy = rcopy(psib.at[n % 2, pl.ds(2 * q, 2)], rd.at[n, pl.ds(2 * q, 2)], ds_s.at[n, q], ds_r.at[n, q], sib)
            copy.start()
            out.append(copy)
        sib_sends[n] = out
        for q in range(4):
            pown[n, 2 * q:2 * q + 2] = merged(c * 4 + q)

    def piece(n, h, zd):
        if n % 2 == 0:
            return pown.at[n, h * 4 + zd]
        return pown.at[n, y * 4 + zd, pl.ds(h * 32, 32)]

    def half_buf(buf, n, i):
        if n % 2 == 0:
            return buf.at[n, i]
        return buf.at[n, i, pl.ds(0, 32)]

    def z_first_sends(n):
        send(piece(n, 0, zo), half_buf(rfar, n, 0), fs_s.at[n, 0], fs_r.at[n, 0], zm)
        send(piece(n, 1, zo), half_buf(rfar, n, 1), fs_s.at[n, 1], fs_r.at[n, 1], zp)
        send(piece(n, 1, zq), half_buf(rnear, n, 0), ns_s.at[n, 0], ns_r.at[n, 0], zm)
        send(piece(n, 0, zn), half_buf(rnear, n, 1), ns_s.at[n, 1], ns_r.at[n, 1], zp)

    def z_second_sends(n):
        for i, zd, dev in ((0, zq, zm), (1, zn, zp)):
            buf = half_buf(rfar, n, i)
            rcopy(buf, buf, fs_s.at[n, i], fs_r.at[n, i], sib).wait_recv()
            dst = piece(n, i, zd)
            dst[...] = dst[...] + buf[...]
        for i, zd, dev in ((0, zq, zm), (1, zn, zp)):
            send(piece(n, i, zd), half_buf(rnear, n, 2 + i), ns_s.at[n, 2 + i], ns_r.at[n, 2 + i], dev)

    def z_total(n):
        for i in range(4):
            buf = half_buf(rnear, n, i)
            rcopy(buf, buf, ns_s.at[n, i], ns_r.at[n, i], sib).wait_recv()
        for h, i, j in ((0, 1, 2), (1, 0, 3)):
            dst = piece(n, h, z)
            dst[...] = dst[...] + half_buf(rnear, n, i)[...] + half_buf(rnear, n, j)[...]

    def core_total(n):
        for q in range(4):
            buf = rd.at[n, pl.ds(2 * q, 2)]
            rcopy(buf, buf, ds_s.at[n, q], ds_r.at[n, q], sib).wait_recv()
            pown[n, 2 * q:2 * q + 2] = pown[n, 2 * q:2 * q + 2] + rd[n, 2 * q:2 * q + 2]

    def y_buf(n):
        return ry.at[n, pl.ds(0, 1)] if n % 2 == 0 else ry.at[n]

    def y_src(n):
        return pown.at[n, pl.ds((1 - y) * 4 + z, 1)] if n % 2 == 0 else pown.at[n, pl.ds((1 - y) * 4, 4)]

    def y_send(n):
        send(y_src(n), y_buf(n), ys_s.at[n], ys_r.at[n], yn)

    def y_wait(n):
        rcopy(y_buf(n), y_buf(n), ys_s.at[n], ys_r.at[n], sib).wait_recv()

    def finish(n, v):
        out_ref[:, n * CW:(n + 1) * CW] = v.astype(bf16)

    def stage(n, j):
        if n % 2 == 0:
            if j == 0:
                core_total(n)
                z_first_sends(n)
            elif j == 1:
                z_second_sends(n)
            elif j == 2:
                z_total(n)
                y_send(n)
            else:
                y_wait(n)
                finish(n, pown[n, y * 4 + z] + ry[n, 0])
        else:
            if j == 0:
                core_total(n)
                y_send(n)
            elif j == 1:
                y_wait(n)
                own = pown.at[n, pl.ds(y * 4, 4)]
                own[...] = own[...] + ry[n]
                z_first_sends(n)
            elif j == 2:
                z_second_sends(n)
            else:
                z_total(n)
                finish(n, pown[n, y * 4 + z])

    for t in range(nc + 3):
        if t < nc:
            down(t)
            combine(t)
        for j in range(4):
            if 0 <= t - j < nc:
                stage(t - j, j)

    for out in sib_sends.values():
        for copy in out:
            copy.wait_send()
    for copy in sends:
        copy.wait_send()


def solution(mesh):
    row_spec = P(("dp", "ep", "tp"), None)

    def local_moe(x, ids, gates, wg, wu, wd):
        rows, d_model = x.shape
        n_exp, _, ff = wg.shape
        nc = d_model // CW
        kw = d_model // NK
        f32, bf16 = jnp.float32, jnp.bfloat16
        vm, dma = pltpu.VMEM, pltpu.SemaphoreType.DMA
        whole = pl.BlockSpec(memory_space=pltpu.VMEM)
        far = pl.BlockSpec(memory_space=pl.ANY)
        return pl.pallas_call(
            moe_kernel,
            out_shape=jax.ShapeDtypeStruct((rows, d_model), bf16),
            in_specs=[whole, whole, whole, far, far, far],
            out_specs=whole,
            scratch_shapes=[
                vm((NK, 16, rows, kw), bf16),
                vm((n_exp, 128, kw), bf16),
                vm((16, 16, 128), f32),
                vm((8, 256, 128), bf16),
                vm((8, 128, 768), bf16),
                vm((n_exp, 128, 128), f32),
                vm((n_exp, 128, ff), f32),
                vm((n_exp, 128, ff), f32),
                vm((n_exp, 128, ff), bf16),
                vm((8 * 768, CW), bf16),
                vm((n_exp // GRP, GRP, kw, ff), bf16),
                vm((n_exp // GRP, GRP, kw, ff), bf16),
                vm((2, n_exp, ff, CW), bf16),
                vm((nc, 8, rows, CW), f32),
                vm((2, 8, rows, CW), f32),
                vm((nc, 8, rows, CW), f32),
                vm((nc, 2, rows, CW), f32),
                vm((nc, 4, rows, CW), f32),
                vm((nc, 4, rows, CW), f32),
                dma((NK, 15)), dma((NK, 16)), dma((15,)), dma((16,)),
                dma((2, n_exp // GRP)), dma((2, n_exp // GRP)),
                dma((nc, 4)), dma((nc, 4)), dma((nc, 2)), dma((nc, 2)),
                dma((nc, 4)), dma((nc, 4)), dma((nc,)), dma((nc,)),
            ],
            compiler_params=pltpu.CompilerParams(
                collective_id=0, has_side_effects=True, vmem_limit_bytes=66_000_000),
        )(x, ids, gates, wg, wu, wd)

    return jax.shard_map(
        local_moe, mesh=mesh,
        in_specs=(row_spec, row_spec, row_spec, P("ep", None, "tp"), P("ep", None, "tp"), P("ep", "tp", None)),
        out_specs=row_spec, check_vma=False)
```

time: 286 us -> 186 us (0.65)
  Pallas kernels: 0 us -> 119 us
  waiting for transfers between devices: 103 us -> 0 us
  blocking collectives: 64.1 us -> 0 us
  other arithmetic: 43.3 us -> 0 us
  local copies, waits for them, and re-layouts: 25.2 us -> 64.8 us
  matrix products: 36.1 us -> 0 us
  between operations: 13.5 us -> 0.01 us
    pallas_call x0 -> x1, Pallas kernels: none -> 119 us  [local_moe(): pl.pallas_call(moe_kernel, out_shape=jax.ShapeDtypeStruct((rows, d_model)...]
    reduce_scatter x1 -> x0, waiting for transfers between devices: 102 us -> none  [local_moe(): lax.psum_scatter(partial_sum, ('ep', 'tp'), scatter_dimension=0, tiled=True)]
    unnamed x0 -> x5, local copies, waits for them, and re-layouts: none -> 64.8 us
    all_gather x2 -> x0, blocking collectives: 64.1 us -> none  [the longest x1 34.8 us: local_moe(): gate_all = lax.all_gather(gate_local, ('ep', 'tp'), tiled=True)]
    dot_general x2 -> x0, matrix products: 36.1 us -> none  [the longest x1 23.2 us: local_moe(): jnp.einsum('ecf,efd->ecd', hidden, w_down, preferred_element_type=jnp.flo...]
    scatter-add x1 -> x0, other arithmetic: 24.8 us -> none  [local_moe(): partial_sum = jax.ops.segment_sum(out_rows, tok_rows, num_segments=num_tok)]
    gather x2 -> x0, local copies, waits for them, and re-layouts: 24 us -> none  [the longest x1 15.5 us: local_moe(): x_rows = x_all[tok_rows].reshape(e_local, expert_cap, -1)]
    mul x1 -> x0, other arithmetic: 9.92 us -> none  [local_moe(): out_rows = out_rows.reshape(local_pairs, -1) * gate_rows[:, None]]
  transfers between devices with their start and end apart: 2 -> 0, of which waited for: 1 -> 0; matrix products, arithmetic and copies ran while one was open for 6% -> 0% of each run, Pallas kernels for 0% -> 0%
where the time goes in v1:
time: 186 us; the launch traced here: 184 us
  Pallas kernels  119 us (64%)
  local copies, waits for them, and re-layouts  64.8 us (35%)
    pallas_call x1, Pallas kernels, local_moe(): pl.pallas_call(moe_kernel, out_shape=jax.ShapeDtypeStruct((rows, d_model)...  119 us
    unnamed x5, local copies, waits for them, and re-layouts  64.8 us

profile of v1, /device:TPU:0, one launch (start us, length us, event | category | flops | bytes accessed | tf_op | source)
XLA Modules:
  0.0 183.8 jit_solution(11081577884364045681)
XLA Ops:
  0.0 1.4 copy.7.ids_ref
  1.4 1.4 copy.8.gate_ref
  2.8 31.3 %copy.9.wg = bf16[16,2048,352]{2,1,0:T(8,128)(2,1)} copy(bf16[16,2048,352]{1,2,0:T(8,128)(2,1)} %param.9) | data formatting | bytes 46137344 | tf_op args[3]
  34.0 29.1 %copy.10.wu = bf16[16,2048,352]{2,1,0:T(8,128)(2,1)} copy(bf16[16,2048,352]{1,2,0:T(8,128)(2,1)} %param.10) | data formatting | bytes 46137344 | tf_op args[4]
  63.1 119.1 %shard_map.64 = bf16[64,2048]{1,0:T(8,128)(2,1)} custom-call(bf16[64,2048]{1,0:T(8,128)(2,1)} %x_ref.1, s32[64,6]{1,0:T(8,128)} %copy.7.ids_ref, f32[64,6]{1,0:T(8,128)} %copy.8.gate_ref, bf16[16,2048,352]{2,1,0:T(8,128)(2,1)} %copy.9.wg, bf16[16,2048,352]{2,1,0:T(8,128)(2,1)} %copy.10.wu, bf16[16,352,2048]{2,1,0:T(8,128)(2,1)} %wd.1), custom_call_target="tpu_custom_call" | custom-call | tf_op jit(solution)/shard_map/pallas_call | solution.py:394
  182.2 1.7 copy.12

commit v2 on v1

v2 whole, which is shorter than its diff:
```python
import functools

import jax
import jax.numpy as jnp
from jax import lax
from jax.experimental import pallas as pl
from jax.experimental.pallas import tpu as pltpu
from jax.sharding import PartitionSpec as P

MESH = pl.DeviceIdType.MESH
NK = 4
CW = 256
GRP = 4
SLOTS = 8
ROWS = 64
TOPK = 6
FLIP = True
ZFIRST = (1,)


def moe_kernel(x_ref, ids_ref, gate_ref, wg, wu, wd, out_ref,
               xall, xg, meta, pmat, cmat, gbuf, acc_a, acc_b, hbuf, obuf,
               wgs, wus, wds, pown, psib, rd, rr, rl, rr2, rl2, ry,
               ags, agr, mss, msr, wsem, wdsem,
               ds_s, ds_r, rr_s, rr_r, rl_s, rl_r, ys_s, ys_r):
    f32, bf16 = jnp.float32, jnp.bfloat16
    d_model = x_ref.shape[1]
    kw = d_model // NK
    nc = d_model // CW
    n_exp = wg.shape[0]
    n_grp = n_exp // GRP

    z = lax.axis_index("tp")
    ep = lax.axis_index("ep")
    y = ep // 2
    c = ep % 2
    sib = {"ep": 2 * y + 1 - c}
    yn = {"ep": 2 * (1 - y) + c}
    sends = []
    hops = []

    def rcopy(src, dst, ssem, rsem, dev):
        return pltpu.make_async_remote_copy(src_ref=src, dst_ref=dst, send_sem=ssem, recv_sem=rsem,
                                            device_id=dev, device_id_type=MESH)

    def send(*args):
        copy = rcopy(*args)
        copy.start()
        sends.append(copy)

    def w_copies(k, g):
        rows = pl.ds(g * GRP, GRP)
        cols = pl.ds(k * kw, kw)
        return (pltpu.make_async_copy(wg.at[rows, :, cols], wgs.at[g], wsem.at[0, g]),
                pltpu.make_async_copy(wu.at[rows, :, cols], wus.at[g], wsem.at[1, g]))

    def wd_copy(n, g):
        rows = pl.ds(g * GRP, GRP)
        return pltpu.make_async_copy(wd.at[rows, :, pl.ds(n * CW, CW)], wds.at[n % 2, rows], wdsem.at[n % 2, g])

    for g in range(n_grp):
        for copy in w_copies(0, g):
            copy.start()
    for n in range(2):
        for g in range(n_grp):
            wd_copy(n, g).start()

    barrier = pltpu.get_barrier_semaphore()
    peers = [{"ep": (ep + d // 4) % 4, "tp": (z + d % 4) % 4} for d in range(1, 16)]
    for peer in peers:
        pl.semaphore_signal(barrier, inc=1, device_id=peer, device_id_type=MESH)
    pl.semaphore_wait(barrier, 15)

    def idx(cc, yy, zz):
        return cc * 8 + yy * 4 + zz

    me = idx(c, y, z)

    def send_block(k, slot, b, dev):
        src = x_ref.at[:, pl.ds(k * kw, kw)] if b is me else xall.at[k, b]
        send(src, xall.at[k, b], ags.at[k, slot], agr.at[k, b], dev)

    def wait_block(k, b):
        rcopy(xall.at[k, b], xall.at[k, b], ags.at[k, 0], agr.at[k, b], sib).wait_recv()

    def z_block(k, i):
        return rcopy(x_ref.at[:, pl.ds(k * kw, kw)], xall.at[k, me], ags.at[k, i], agr.at[k, me],
                     {"tp": (z + i) % 4})

    def relay(k):
        b = idx(c, y, 3 * (2 - z))
        return rcopy(xall.at[k, b], xall.at[k, b], ags.at[k, 15], agr.at[k, b], {"tp": 3 * (z - 1)})

    inner = (z == 1) | (z == 2)
    near = {1: z < 3, 2: None, 3: z > 0}

    def send_z(k):
        for i in (2, 1, 3):
            if near[i] is None:
                copy = z_block(k, i)
                copy.start()
                sends.append(copy)
            else:
                pl.when(near[i])(lambda: z_block(k, i).start())
                hops.append((near[i], [functools.partial(z_block, k, i)]))

    def send_own(k):
        send_block(k, 0, me, yn)
        send_block(k, 4, me, sib)

    def step_a(k):
        for i in (2, 1, 3):
            b = idx(c, y, (z + i) % 4)
            wait_block(k, b)
            if i == 2:
                pl.when(inner)(lambda: relay(k).start())
                hops.append((inner, [functools.partial(relay, k)]))
                if k + 1 < NK:
                    send_z(k + 1)
            send_block(k, 4 + i, b, yn)
            send_block(k, 7 + i, b, sib)
        if k + 2 < NK:
            send_own(k + 2)

    def step_b(k):
        for i in range(4):
            b = idx(c, 1 - y, (z + i) % 4)
            wait_block(k, b)
            send_block(k, 11 + i, b, sib)

    def wait_sibling(k):
        for b in range(8):
            wait_block(k, (1 - c) * 8 + b)

    send_z(0)
    send_own(0)

    lane = lax.broadcasted_iota(jnp.int32, (128, 128), 1)
    sub = lax.broadcasted_iota(jnp.int32, (128, 128), 0)
    tri = jnp.where((sub < lane % ROWS) & (sub < ROWS), 1.0, 0.0).astype(bf16)

    def twice(v):
        v = jnp.concatenate([v, v], axis=1)
        return jnp.concatenate([v, jnp.zeros((8 - TOPK, 128), f32)], axis=0)

    ids_t = twice(ids_ref[...].astype(f32))
    gate_t = twice(gate_ref[...])
    exp_id = lax.broadcasted_iota(jnp.int32, (64, 128), 0).astype(f32)
    hits = [jnp.where(exp_id == ids_t[j:j + 1], 1.0, 0.0) for j in range(TOPK)]
    chosen = functools.reduce(lambda p, q: p + q, hits)
    rank = jnp.dot(chosen.astype(bf16), tri, preferred_element_type=f32)
    code = [SLOTS * ids_t[j:j + 1] + jnp.sum(rank * hits[j], axis=0, keepdims=True) for j in range(TOPK)]
    code = jnp.concatenate(code + [jnp.full((8 - TOPK, 128), -1.0, f32)], axis=0)
    meta[me, 0:8, :] = code
    meta[me, 8:16, :] = gate_t
    for k in range(NK):
        xall[k, me] = x_ref[:, k * kw:(k + 1) * kw]
    for d, peer in enumerate(peers):
        send(meta.at[me], meta.at[me], mss.at[d], msr.at[me], peer)
    if NK > 1:
        send_own(1)

    step_a(0)

    for d in range(1, 16):
        s_ep, s_z = (ep + d // 4) % 4, (z + d % 4) % 4
        b = idx(s_ep % 2, s_ep // 2, s_z)
        rcopy(meta.at[b], meta.at[b], mss.at[0], msr.at[b], sib).wait_recv()

    def build(p, carry):
        half = lax.broadcasted_iota(jnp.int32, (8, 128), 1) < ROWS
        both = jnp.where(half, meta[2 * p, 0:8, :], meta[2 * p + 1, 0:8, :]).astype(jnp.int32)
        gts = jnp.where(half, meta[2 * p, 8:16, :], meta[2 * p + 1, 8:16, :])
        expert = lax.shift_right_arithmetic(both, 3)
        slot = both - expert * SLOTS
        row = (expert - ep * n_exp) * (2 * SLOTS) + jnp.where(half, 0, SLOTS) + slot
        r = lax.broadcasted_iota(jnp.int32, (n_exp * 2 * SLOTS, 128), 0)
        sel = jnp.zeros(r.shape, f32)
        wts = jnp.zeros(r.shape, f32)
        for j in range(TOPK):
            eq = r == row[j:j + 1]
            sel = jnp.where(eq, 1.0, sel)
            wts = jnp.where(eq, gts[j:j + 1], wts)
        pmat[p] = sel.astype(bf16)
        selt = sel.T.astype(bf16)
        cmat[p] = jnp.concatenate([selt, selt, selt], axis=1)
        per_row = jnp.broadcast_to(jnp.sum(wts, axis=1, keepdims=True), wts.shape)
        for e in range(n_exp):
            gbuf[e, pl.ds(p * 16, 16), :] = per_row[e * 16:(e + 1) * 16]
        return carry

    lax.fori_loop(0, 8, build, 0)
    if NK > 1:
        step_a(1)
    step_b(0)

    def proj(w, xe):
        dims = (((1,), (1,)), ((), ()))
        if FLIP:
            return lax.dot_general(w, xe, dims, preferred_element_type=f32)
        return lax.dot_general(xe, w, dims, preferred_element_type=f32)

    def compute(k, between):
        def gather(i, carry):
            for u in range(2):
                p = i * 2 + u
                rows = xall[k, pl.ds(2 * p, 2)].reshape(2 * ROWS, kw)
                v = jnp.dot(pmat[p], rows, preferred_element_type=f32).astype(bf16)
                for e in range(n_exp):
                    xg[e, pl.ds(p * 16, 16), :] = v[e * 16:(e + 1) * 16]
            return carry

        lax.fori_loop(0, 4, gather, 0)

        def experts(g, carry):
            for copy in w_copies(k, g):
                copy.wait()
            for u in range(GRP):
                e = g * GRP + u
                xe = xg[e]
                a = proj(wgs[g, u], xe)
                b = proj(wus[g, u], xe)
                if k > 0:
                    a = acc_a[e] + a
                    b = acc_b[e] + b
                if k < NK - 1:
                    acc_a[e] = a
                    acc_b[e] = b
                else:
                    h = jax.nn.silu(a) * b
                    hbuf[e] = (h.T if FLIP else h).astype(bf16)
            if k < NK - 1:
                for copy in w_copies(k + 1, g):
                    copy.start()
            return carry

        lax.fori_loop(0, n_grp // 2, experts, 0)
        between()
        lax.fori_loop(n_grp // 2, n_grp, experts, 0)

    for k in range(NK):
        wait_sibling(k)
        compute(k, functools.partial(step_a, k + 2) if k + 2 < NK else lambda: None)
        if k + 1 < NK:
            step_b(k + 1)

    def down(n):
        def body(g, carry):
            wd_copy(n, g).wait()
            for u in range(GRP):
                e = g * GRP + u
                o = jnp.dot(hbuf[e], wds[n % 2, e], preferred_element_type=f32)
                gt = gbuf[e]
                o = o * jnp.concatenate([gt] * (CW // 128), axis=1)
                parts = []
                for i in range(3):
                    part = o.astype(bf16)
                    if i < 2:
                        o = o - part.astype(f32)
                    parts.append(part)
                for p in range(8):
                    for i in range(3):
                        obuf[pl.ds(p * 768 + i * 256 + e * 16, 16), :] = parts[i][p * 16:(p + 1) * 16]
            return carry

        lax.fori_loop(0, n_grp, body, 0)
        if n + 2 < nc:
            for g in range(n_grp):
                wd_copy(n + 2, g).start()

    def merged(p):
        v = jnp.dot(cmat[p], obuf[pl.ds(p * 768, 768), :], preferred_element_type=f32)
        return v.reshape(2, ROWS, CW)

    def part(ref, n, q):
        return ref.at[n, pl.ds(2 * (q % 2), 2), q // 2]

    sib_sends = {}

    def combine(n):
        if n >= 2:
            for copy in sib_sends.pop(n - 2):
                copy.wait_send()
        out = []
        for q in range(4):
            part(psib, n % 2, q)[...] = merged((1 - c) * 4 + q)
        for q in range(4):
            copy = rcopy(part(psib, n % 2, q), part(rd, n, q), ds_s.at[n, q], ds_r.at[n, q], sib)
            copy.start()
            out.append(copy)
        sib_sends[n] = out
        for q in range(4):
            part(pown, n, q)[...] = merged(c * 4 + q)

    def add(dst, src):
        dst[...] = dst[...] + src[...]

    def core_total(n):
        for q in range(4):
            buf = part(rd, n, q)
            rcopy(buf, buf, ds_s.at[n, q], ds_r.at[n, q], sib).wait_recv()
            add(part(pown, n, q), buf)

    def piece(n, d):
        return pown.at[n, d] if n in ZFIRST else pown.at[n, d, y]

    def r_buf(n, d):
        return rr2.at[ZFIRST.index(n), d] if n in ZFIRST else rr.at[n, d]

    def l_buf(n, d):
        return rl2.at[ZFIRST.index(n), d] if n in ZFIRST else rl.at[n, d]

    def hop(n, at, right):
        buf, ssem, rsem = (r_buf, rr_s, rr_r) if right else (l_buf, rl_s, rl_r)
        dests = range(3, at, -1) if right else range(0, at)
        here = z == at

        def onward(n, d):
            return rcopy(piece(n, d), buf(n, d), ssem.at[n, d], rsem.at[n, d],
                         {"tp": (z + (1 if right else 3)) % 4})

        @pl.when(here)
        def _():
            for d in dests:
                if 0 < at < 3:
                    rcopy(buf(n, d), buf(n, d), ssem.at[n, d], rsem.at[n, d], sib).wait_recv()
                    add(piece(n, d), buf(n, d))
                onward(n, d).start()

        hops.append((here, [functools.partial(onward, n, d) for d in dests]))

    def z_total(n):
        @pl.when(z > 0)
        def _():
            rcopy(r_buf(n, z), r_buf(n, z), rr_s.at[n, z], rr_r.at[n, z], sib).wait_recv()
            add(piece(n, z), r_buf(n, z))

        @pl.when(z < 3)
        def _():
            rcopy(l_buf(n, z), l_buf(n, z), rl_s.at[n, z], rl_r.at[n, z], sib).wait_recv()
            add(piece(n, z), l_buf(n, z))

    def y_buf(n):
        return ry.at[n, pl.ds(0, 1)] if n in ZFIRST else ry.at[n]

    def y_send(n):
        src = pown.at[n, pl.ds(z, 1), 1 - y] if n in ZFIRST else pown.at[n, :, 1 - y]
        send(src, y_buf(n), ys_s.at[n], ys_r.at[n], yn)

    def y_add(n):
        rcopy(y_buf(n), y_buf(n), ys_s.at[n], ys_r.at[n], sib).wait_recv()
        add(pown.at[n, pl.ds(z, 1), y] if n in ZFIRST else pown.at[n, :, y], y_buf(n))

    def finish(n):
        out_ref[:, n * CW:(n + 1) * CW] = pown[n, z, y].astype(bf16)

    def y_hop(n):
        y_add(n)
        hop(n, 0, True)
        hop(n, 3, False)

    def hop_1(n):
        hop(n, 1, True)
        hop(n, 2, False)

    def hop_2(n):
        hop(n, 2, True)
        hop(n, 1, False)

    def z_end(n):
        z_total(n)
        if n in ZFIRST:
            y_send(n)
        else:
            finish(n)

    def y_end(n):
        y_add(n)
        finish(n)

    def first(n):
        core_total(n)
        if n in ZFIRST:
            hop(n, 0, True)
            hop(n, 3, False)
        else:
            y_send(n)

    stages = {False: {2: y_hop, 3: hop_1, 4: hop_2, 5: z_end},
              True: {2: hop_1, 3: hop_2, 4: z_end, 6: y_end}}
    for t in range(nc + 6):
        if t < nc:
            down(t)
            combine(t)
        for lag in range(6, 0, -1):
            n = t - lag
            if 0 <= n < nc and lag in stages[n in ZFIRST]:
                stages[n in ZFIRST][lag](n)
        if t < nc:
            first(t)

    for out in sib_sends.values():
        for copy in out:
            copy.wait_send()
    for copy in sends:
        copy.wait_send()
    for here, makers in hops:
        @pl.when(here)
        def _():
            for maker in makers:
                maker().wait_send()


def solution(mesh):
    row_spec = P(("dp", "ep", "tp"), None)

    def local_moe(x, ids, gates, wg, wu, wd):
        rows, d_model = x.shape
        n_exp, _, ff = wg.shape
        nc = d_model // CW
        kw = d_model // NK
        f32, bf16 = jnp.float32, jnp.bfloat16
        vm, dma = pltpu.VMEM, pltpu.SemaphoreType.DMA
        whole = pl.BlockSpec(memory_space=pltpu.VMEM)
        far = pl.BlockSpec(memory_space=pl.ANY)
        return pl.pallas_call(
            moe_kernel,
            out_shape=jax.ShapeDtypeStruct((rows, d_model), bf16),
            in_specs=[whole, whole, whole, far, far, far],
            out_specs=whole,
            scratch_shapes=[
                vm((NK, 16, rows, kw), bf16),
                vm((n_exp, 128, kw), bf16),
                vm((16, 16, 128), f32),
                vm((8, 256, 128), bf16),
                vm((8, 128, 768), bf16),
                vm((n_exp, 128, 128), f32),
                vm((n_exp, ff, 128) if FLIP else (n_exp, 128, ff), f32),
                vm((n_exp, ff, 128) if FLIP else (n_exp, 128, ff), f32),
                vm((n_exp, 128, ff), bf16),
                vm((8 * 768, CW), bf16),
                vm((n_exp // GRP, GRP, ff, kw), bf16),
                vm((n_exp // GRP, GRP, ff, kw), bf16),
                vm((2, n_exp, ff, CW), bf16),
                vm((nc, 4, 2, rows, CW), f32),
                vm((2, 4, 2, rows, CW), f32),
                vm((nc, 4, 2, rows, CW), f32),
                vm((nc, 4, rows, CW), f32),
                vm((nc, 4, rows, CW), f32),
                vm((len(ZFIRST), 4, 2, rows, CW), f32),
                vm((len(ZFIRST), 4, 2, rows, CW), f32),
                vm((nc, 4, rows, CW), f32),
                dma((NK, 16)), dma((NK, 16)), dma((15,)), dma((16,)),
                dma((2, n_exp // GRP)), dma((2, n_exp // GRP)),
                dma((nc, 4)), dma((nc, 4)), dma((nc, 4)), dma((nc, 4)),
                dma((nc, 4)), dma((nc, 4)), dma((nc,)), dma((nc,)),
            ],
            compiler_params=pltpu.CompilerParams(
                collective_id=0, has_side_effects=True, vmem_limit_bytes=66_000_000),
        )(x, ids.T, gates.T, wg.swapaxes(1, 2), wu.swapaxes(1, 2), wd)

    return jax.shard_map(
        local_moe, mesh=mesh,
        in_specs=(row_spec, row_spec, row_spec, P("ep", None, "tp"), P("ep", None, "tp"), P("ep", "tp", None)),
        out_specs=row_spec, check_vma=False)
```

time: 186 us -> 118 us (0.63); the launches traced: 184 us -> 118 us
  local copies, waits for them, and re-layouts: 64.8 us -> 1.67 us
  Pallas kernels: 119 us -> 116 us
    unnamed x5 -> x1, local copies, waits for them, and re-layouts: 64.8 us -> 1.67 us
    pallas_call x1, Pallas kernels: 119 us -> 116 us  [local_moe(): pl.pallas_call(moe_kernel, out_shape=jax.ShapeDtypeStruct((rows, d_model)...]
where the time goes in v2:
time: 118 us
  Pallas kernels  116 us (98%)
  local copies, waits for them, and re-layouts  1.67 us (1%)
    pallas_call x1, Pallas kernels, local_moe(): pl.pallas_call(moe_kernel, out_shape=jax.ShapeDtypeStruct((rows, d_model)...  116 us

profile of v2, /device:TPU:0, one launch (start us, length us, event | category | flops | bytes accessed | tf_op | source)
XLA Modules:
  0.0 118.0 jit_solution(13777281777183010776)
XLA Ops:
  0.0 116.3 %shard_map.64 = bf16[64,2048]{1,0:T(8,128)(2,1)} custom-call(bf16[64,2048]{1,0:T(8,128)(2,1)} %x_ref.1, s32[6,64]{1,0:T(8,128)} %bitcast.6, f32[6,64]{1,0:T(8,128)} %bitcast.7, bf16[16,352,2048]{2,1,0:T(8,128)(2,1)} %bitcast.4, bf16[16,352,2048]{2,1,0:T(8,128)(2,1)} %bitcast.5, bf16[16,352,2048]{2,1,0:T(8,128)(2,1)} %wd.1), custom_call_target="tpu_custom_call" | custom-call | tf_op jit(solution)/shard_map/pallas_call | solution.py:426
  116.3 1.7 %copy.8 = bf16[64,2048]{1,0:T(8,128)(2,1)} copy(bf16[64,2048]{1,0:T(8,128)(2,1)} %shard_map.64) | data formatting | bytes 524288

commit v3 on v2

--- a/solution.py
+++ b/solution.py
@@ -8,13 +8,17 @@
 from jax.sharding import PartitionSpec as P
 
 MESH = pl.DeviceIdType.MESH
-NK = 4
+NK = 8
+STEPS = ((0, 1), (1, 2), (3, 2), (5, 2), (7, 1))
 CW = 256
-GRP = 4
+WIDTHS = (256,) * 8
+GRP = 8
 SLOTS = 8
 ROWS = 64
 TOPK = 6
+AHEAD = 3
 FLIP = True
+DIRECT = (7,)
 ZFIRST = (1,)
 
 
@@ -26,7 +30,8 @@
     f32, bf16 = jnp.float32, jnp.bfloat16
     d_model = x_ref.shape[1]
     kw = d_model // NK
-    nc = d_model // CW
+    nc = len(WIDTHS)
+    starts = [sum(WIDTHS[:n]) for n in range(nc)]
     n_exp = wg.shape[0]
     n_grp = n_exp // GRP
 
@@ -48,15 +53,17 @@
         copy.start()
         sends.append(copy)
 
-    def w_copies(k, g):
+    def w_copies(s, g):
         rows = pl.ds(g * GRP, GRP)
-        cols = pl.ds(k * kw, kw)
-        return (pltpu.make_async_copy(wg.at[rows, :, cols], wgs.at[g], wsem.at[0, g]),
-                pltpu.make_async_copy(wu.at[rows, :, cols], wus.at[g], wsem.at[1, g]))
+        cols = pl.ds(STEPS[s][0] * kw, STEPS[s][1] * kw)
+        here = pl.ds(0, STEPS[s][1] * kw)
+        return (pltpu.make_async_copy(wg.at[rows, :, cols], wgs.at[g, :, :, here], wsem.at[0, g]),
+                pltpu.make_async_copy(wu.at[rows, :, cols], wus.at[g, :, :, here], wsem.at[1, g]))
 
     def wd_copy(n, g):
         rows = pl.ds(g * GRP, GRP)
-        return pltpu.make_async_copy(wd.at[rows, :, pl.ds(n * CW, CW)], wds.at[n % 2, rows], wdsem.at[n % 2, g])
+        return pltpu.make_async_copy(wd.at[rows, :, pl.ds(starts[n], WIDTHS[n])],
+                                     wds.at[n % 2, rows, :, pl.ds(0, WIDTHS[n])], wdsem.at[n % 2, g])
 
     for g in range(n_grp):
         for copy in w_copies(0, g):
@@ -115,12 +122,10 @@
             if i == 2:
                 pl.when(inner)(lambda: relay(k).start())
                 hops.append((inner, [functools.partial(relay, k)]))
-                if k + 1 < NK:
-                    send_z(k + 1)
+                if k + AHEAD < NK:
+                    send_z(k + AHEAD)
             send_block(k, 4 + i, b, yn)
             send_block(k, 7 + i, b, sib)
-        if k + 2 < NK:
-            send_own(k + 2)
 
     def step_b(k):
         for i in range(4):
@@ -157,8 +162,10 @@
         xall[k, me] = x_ref[:, k * kw:(k + 1) * kw]
     for d, peer in enumerate(peers):
         send(meta.at[me], meta.at[me], mss.at[d], msr.at[me], peer)
-    if NK > 1:
-        send_own(1)
+    for k in range(1, NK):
+        if k < AHEAD:
+            send_z(k)
+        send_own(k)
 
     step_a(0)
 
@@ -185,14 +192,10 @@
         selt = sel.T.astype(bf16)
         cmat[p] = jnp.concatenate([selt, selt, selt], axis=1)
         per_row = jnp.broadcast_to(jnp.sum(wts, axis=1, keepdims=True), wts.shape)
-        for e in range(n_exp):
-            gbuf[e, pl.ds(p * 16, 16), :] = per_row[e * 16:(e + 1) * 16]
+        gbuf[:, pl.ds(p * 16, 16), :] = per_row.reshape(n_exp, 16, 128)
         return carry
 
     lax.fori_loop(0, 8, build, 0)
-    if NK > 1:
-        step_a(1)
-    step_b(0)
 
     def proj(w, xe):
         dims = (((1,), (1,)), ((), ()))
@@ -200,67 +203,92 @@
             return lax.dot_general(w, xe, dims, preferred_element_type=f32)
         return lax.dot_general(xe, w, dims, preferred_element_type=f32)
 
-    def compute(k, between):
+    def compute(s, *between):
+        k0, count = STEPS[s]
+        width = count * kw
+
         def gather(i, carry):
             for u in range(2):
                 p = i * 2 + u
-                rows = xall[k, pl.ds(2 * p, 2)].reshape(2 * ROWS, kw)
-                v = jnp.dot(pmat[p], rows, preferred_element_type=f32).astype(bf16)
-                for e in range(n_exp):
-                    xg[e, pl.ds(p * 16, 16), :] = v[e * 16:(e + 1) * 16]
+                for j in range(count):
+                    rows = xall[k0 + j, pl.ds(2 * p, 2)].reshape(2 * ROWS, kw)
+                    v = jnp.dot(pmat[p], rows, preferred_element_type=f32).astype(bf16)
+                    xg[:, pl.ds(p * 16, 16), j * kw:(j + 1) * kw] = v.reshape(n_exp, 16, kw)
             return carry
 
         lax.fori_loop(0, 4, gather, 0)
 
         def experts(g, carry):
-            for copy in w_copies(k, g):
+            for copy in w_copies(s, g):
                 copy.wait()
             for u in range(GRP):
                 e = g * GRP + u
-                xe = xg[e]
-                a = proj(wgs[g, u], xe)
-                b = proj(wus[g, u], xe)
-                if k > 0:
+                xe = xg[e, :, 0:width]
+                a = proj(wgs[g, u, :, 0:width], xe)
+                b = proj(wus[g, u, :, 0:width], xe)
+                if s > 0:
                     a = acc_a[e] + a
                     b = acc_b[e] + b
-                if k < NK - 1:
+                if s < len(STEPS) - 1:
                     acc_a[e] = a
                     acc_b[e] = b
                 else:
                     h = jax.nn.silu(a) * b
                     hbuf[e] = (h.T if FLIP else h).astype(bf16)
-            if k < NK - 1:
-                for copy in w_copies(k + 1, g):
+            if s < len(STEPS) - 1:
+                for copy in w_copies(s + 1, g):
                     copy.start()
             return carry
 
-        lax.fori_loop(0, n_grp // 2, experts, 0)
-        between()
-        lax.fori_loop(n_grp // 2, n_grp, experts, 0)
-
-    for k in range(NK):
-        wait_sibling(k)
-        compute(k, functools.partial(step_a, k + 2) if k + 2 < NK else lambda: None)
-        if k + 1 < NK:
-            step_b(k + 1)
+        if between:
+            lax.fori_loop(0, n_grp // 2, experts, 0)
+            between[0]()
+            lax.fori_loop(n_grp // 2, n_grp, experts, 0)
+        else:
+            lax.fori_loop(0, n_grp, experts, 0)
+        for step in between[1:]:
+            step()
+
+    def chunks(step, *ks):
+        def run():
+            for k in ks:
+                step(k)
+        return run
+
+    for k in (1, 2): step_a(k)
+    step_b(0)
+    wait_sibling(0)
+    compute(0, chunks(step_a, 3), chunks(step_b, 1))
+    step_a(4)
+    step_b(2)
+    chunks(wait_sibling, 1, 2)()
+    compute(1, chunks(step_a, 5), chunks(step_b, 3))
+    step_a(6)
+    step_b(4)
+    chunks(wait_sibling, 3, 4)()
+    compute(2, chunks(step_a, 7), chunks(step_b, 5))
+    step_b(6)
+    chunks(wait_sibling, 5, 6)()
+    compute(3, chunks(step_b, 7))
+    wait_sibling(7)
+    compute(4)
 
     def down(n):
         def body(g, carry):
             wd_copy(n, g).wait()
             for u in range(GRP):
                 e = g * GRP + u
-                o = jnp.dot(hbuf[e], wds[n % 2, e], preferred_element_type=f32)
+                o = jnp.dot(hbuf[e], wds[n % 2, e, :, 0:WIDTHS[n]], preferred_element_type=f32)
                 gt = gbuf[e]
-                o = o * jnp.concatenate([gt] * (CW // 128), axis=1)
+                o = o * jnp.concatenate([gt] * (WIDTHS[n] // 128), axis=1)
                 parts = []
                 for i in range(3):
                     part = o.astype(bf16)
                     if i < 2:
                         o = o - part.astype(f32)
                     parts.append(part)
-                for p in range(8):
-                    for i in range(3):
-                        obuf[pl.ds(p * 768 + i * 256 + e * 16, 16), :] = parts[i][p * 16:(p + 1) * 16]
+                for i in range(3):
+                    obuf[:, i, e, :, 0:WIDTHS[n]] = parts[i].reshape(8, 16, WIDTHS[n])
             return carry
 
         lax.fori_loop(0, n_grp, body, 0)
@@ -268,12 +296,15 @@
             for g in range(n_grp):
                 wd_copy(n + 2, g).start()
 
-    def merged(p):
-        v = jnp.dot(cmat[p], obuf[pl.ds(p * 768, 768), :], preferred_element_type=f32)
-        return v.reshape(2, ROWS, CW)
-
-    def part(ref, n, q):
-        return ref.at[n, pl.ds(2 * (q % 2), 2), q // 2]
+    def merged(n, p):
+        v = jnp.dot(cmat[p], obuf[p, :, :, :, 0:WIDTHS[n]].reshape(768, WIDTHS[n]), preferred_element_type=f32)
+        return v.reshape(2, ROWS, WIDTHS[n])
+
+    def cols(n):
+        return pl.ds(0, WIDTHS[n])
+
+    def part(ref, n, slot, q):
+        return ref.at[slot, pl.ds(2 * (q % 2), 2), q // 2, :, cols(n)]
 
     sib_sends = {}
 
@@ -283,32 +314,32 @@
                 copy.wait_send()
         out = []
         for q in range(4):
-            part(psib, n % 2, q)[...] = merged((1 - c) * 4 + q)
+            part(psib, n, n % 2, q)[...] = merged(n, (1 - c) * 4 + q)
         for q in range(4):
-            copy = rcopy(part(psib, n % 2, q), part(rd, n, q), ds_s.at[n, q], ds_r.at[n, q], sib)
+            copy = rcopy(part(psib, n, n % 2, q), part(rd, n, n, q), ds_s.at[n, q], ds_r.at[n, q], sib)
             copy.start()
             out.append(copy)
         sib_sends[n] = out
         for q in range(4):
-            part(pown, n, q)[...] = merged(c * 4 + q)
+            part(pown, n, n, q)[...] = merged(n, c * 4 + q)
 
     def add(dst, src):
         dst[...] = dst[...] + src[...]
 
     def core_total(n):
         for q in range(4):
-            buf = part(rd, n, q)
+            buf = part(rd, n, n, q)
             rcopy(buf, buf, ds_s.at[n, q], ds_r.at[n, q], sib).wait_recv()
-            add(part(pown, n, q), buf)
+            add(part(pown, n, n, q), buf)
 
     def piece(n, d):
-        return pown.at[n, d] if n in ZFIRST else pown.at[n, d, y]
+        return pown.at[n, d] if n in ZFIRST else pown.at[n, d, y, :, cols(n)]
 
     def r_buf(n, d):
-        return rr2.at[ZFIRST.index(n), d] if n in ZFIRST else rr.at[n, d]
+        return rr2.at[ZFIRST.index(n), d] if n in ZFIRST else rr.at[n, d, :, cols(n)]
 
     def l_buf(n, d):
-        return rl2.at[ZFIRST.index(n), d] if n in ZFIRST else rl.at[n, d]
+        return rl2.at[ZFIRST.index(n), d] if n in ZFIRST else rl.at[n, d, :, cols(n)]
 
     def hop(n, at, right):
         buf, ssem, rsem = (r_buf, rr_s, rr_r) if right else (l_buf, rl_s, rl_r)
@@ -341,18 +372,18 @@
             add(piece(n, z), l_buf(n, z))
 
     def y_buf(n):
-        return ry.at[n, pl.ds(0, 1)] if n in ZFIRST else ry.at[n]
+        return ry.at[n, pl.ds(0, 1)] if n in ZFIRST else ry.at[n, :, :, cols(n)]
 
     def y_send(n):
-        src = pown.at[n, pl.ds(z, 1), 1 - y] if n in ZFIRST else pown.at[n, :, 1 - y]
+        src = pown.at[n, pl.ds(z, 1), 1 - y] if n in ZFIRST else pown.at[n, :, 1 - y, :, cols(n)]
         send(src, y_buf(n), ys_s.at[n], ys_r.at[n], yn)
 
     def y_add(n):
         rcopy(y_buf(n), y_buf(n), ys_s.at[n], ys_r.at[n], sib).wait_recv()
-        add(pown.at[n, pl.ds(z, 1), y] if n in ZFIRST else pown.at[n, :, y], y_buf(n))
+        add(pown.at[n, pl.ds(z, 1), y] if n in ZFIRST else pown.at[n, :, y, :, cols(n)], y_buf(n))
 
     def finish(n):
-        out_ref[:, n * CW:(n + 1) * CW] = pown[n, z, y].astype(bf16)
+        out_ref[:, starts[n]:starts[n] + WIDTHS[n]] = pown[n, z, y, :, 0:WIDTHS[n]].astype(bf16)
 
     def y_hop(n):
         y_add(n)
@@ -366,6 +397,24 @@
     def hop_2(n):
         hop(n, 2, True)
         hop(n, 1, False)
+
+    def straight(n, i):
+        d = (z + i) % 4
+        return rcopy(piece(n, d), rr.at[n, z, :, cols(n)], rr_s.at[n, i], rr_r.at[n, z], {"tp": d})
+
+    def y_straight(n):
+        y_add(n)
+        for i in (2, 1, 3):
+            copy = straight(n, i)
+            copy.start()
+            sends.append(copy)
+
+    def straight_end(n):
+        for i in (1, 3, 2):
+            buf = r_buf(n, (z + i) % 4)
+            rcopy(buf, buf, rr_s.at[n, i], rr_r.at[n, (z + i) % 4], sib).wait_recv()
+            add(piece(n, z), buf)
+        finish(n)
 
     def z_end(n):
         z_total(n)
@@ -386,16 +435,17 @@
         else:
             y_send(n)
 
-    stages = {False: {2: y_hop, 3: hop_1, 4: hop_2, 5: z_end},
-              True: {2: hop_1, 3: hop_2, 4: z_end, 6: y_end}}
+    plan = {n: {2: y_hop, 3: hop_1, 4: hop_2, 5: z_end} for n in range(nc)}
+    plan.update({n: {2: hop_1, 3: hop_2, 4: z_end, 6: y_end} for n in ZFIRST})
+    plan.update({n: {2: y_straight, 3: straight_end} for n in DIRECT})
     for t in range(nc + 6):
         if t < nc:
             down(t)
             combine(t)
         for lag in range(6, 0, -1):
             n = t - lag
-            if 0 <= n < nc and lag in stages[n in ZFIRST]:
-                stages[n in ZFIRST][lag](n)
+            if 0 <= n < nc and lag in plan[n]:
+                plan[n][lag](n)
         if t < nc:
             first(t)
 
@@ -417,7 +467,7 @@
     def local_moe(x, ids, gates, wg, wu, wd):
         rows, d_model = x.shape
         n_exp, _, ff = wg.shape
-        nc = d_model // CW
+        nc = len(WIDTHS)
         kw = d_model // NK
         f32, bf16 = jnp.float32, jnp.bfloat16
         vm, dma = pltpu.VMEM, pltpu.SemaphoreType.DMA
@@ -430,7 +480,7 @@
             out_specs=whole,
             scratch_shapes=[
                 vm((NK, 16, rows, kw), bf16),
-                vm((n_exp, 128, kw), bf16),
+                vm((n_exp, 128, 2 * kw), bf16),
                 vm((16, 16, 128), f32),
                 vm((8, 256, 128), bf16),
                 vm((8, 128, 768), bf16),
@@ -438,9 +488,9 @@
                 vm((n_exp, ff, 128) if FLIP else (n_exp, 128, ff), f32),
                 vm((n_exp, ff, 128) if FLIP else (n_exp, 128, ff), f32),
                 vm((n_exp, 128, ff), bf16),
-                vm((8 * 768, CW), bf16),
-                vm((n_exp // GRP, GRP, ff, kw), bf16),
-                vm((n_exp // GRP, GRP, ff, kw), bf16),
+                vm((8, 3, n_exp, 16, CW), bf16),
+                vm((n_exp // GRP, GRP, ff, 2 * kw), bf16),
+                vm((n_exp // GRP, GRP, ff, 2 * kw), bf16),
                 vm((2, n_exp, ff, CW), bf16),
                 vm((nc, 4, 2, rows, CW), f32),
                 vm((2, 4, 2, rows, CW), f32),

time: 118 us -> 113 us (0.958)
  Pallas kernels: 116 us -> 111 us
    pallas_call x1, Pallas kernels: 116 us -> 111 us  [local_moe(): pl.pallas_call(moe_kernel, out_shape=jax.ShapeDtypeStruct((rows, d_model)...]
where the time goes in v3:
time: 113 us; the launch traced here: 112 us
  Pallas kernels  111 us (98%)
  local copies, waits for them, and re-layouts  1.67 us (1%)
    pallas_call x1, Pallas kernels, local_moe(): pl.pallas_call(moe_kernel, out_shape=jax.ShapeDtypeStruct((rows, d_model)...  111 us

profile of v3, /device:TPU:0, one launch (start us, length us, event | category | flops | bytes accessed | tf_op | source)
XLA Modules:
  0.0 112.4 jit_solution(2272866874741881332)
XLA Ops:
  0.0 110.7 %shard_map.64 = bf16[64,2048]{1,0:T(8,128)(2,1)} custom-call(bf16[64,2048]{1,0:T(8,128)(2,1)} %x_ref.1, s32[6,64]{1,0:T(8,128)} %bitcast.6, f32[6,64]{1,0:T(8,128)} %bitcast.7, bf16[16,352,2048]{2,1,0:T(8,128)(2,1)} %bitcast.4, bf16[16,352,2048]{2,1,0:T(8,128)(2,1)} %bitcast.5, bf16[16,352,2048]{2,1,0:T(8,128)(2,1)} %wd.1), custom_call_target="tpu_custom_call" | custom-call | tf_op jit(solution)/shard_map/pallas_call | solution.py:476
  110.7 1.7 %copy.8 = bf16[64,2048]{1,0:T(8,128)(2,1)} copy(bf16[64,2048]{1,0:T(8,128)(2,1)} %shard_map.64) | data formatting | bytes 524288

commit v4 on v3

--- a/solution.py
+++ b/solution.py
@@ -22,8 +22,8 @@
 ZFIRST = (1,)
 
 
-def moe_kernel(x_ref, ids_ref, gate_ref, wg, wu, wd, out_ref,
-               xall, xg, meta, pmat, cmat, gbuf, acc_a, acc_b, hbuf, obuf,
+def moe_kernel(x_hbm, ids_hbm, gate_hbm, wg, wu, wd, out_hbm,
+               x_ref, ids_ref, gate_ref, out_ref, in_sem, out_sem, xall, xg, meta, pmat, cmat, gbuf, acc_a, acc_b, hbuf, obuf,
                wgs, wus, wds, pown, psib, rd, rr, rl, rr2, rl2, ry,
                ags, agr, mss, msr, wsem, wdsem,
                ds_s, ds_r, rr_s, rr_r, rl_s, rl_r, ys_s, ys_r):
@@ -65,6 +65,10 @@
         return pltpu.make_async_copy(wd.at[rows, :, pl.ds(starts[n], WIDTHS[n])],
                                      wds.at[n % 2, rows, :, pl.ds(0, WIDTHS[n])], wdsem.at[n % 2, g])
 
+    loads = [pltpu.make_async_copy(src, dst, in_sem.at[i]) for i, (src, dst) in
+             enumerate(((x_hbm, x_ref), (ids_hbm, ids_ref), (gate_hbm, gate_ref)))]
+    for copy in loads:
+        copy.start()
     for g in range(n_grp):
         for copy in w_copies(0, g):
             copy.start()
@@ -76,6 +80,8 @@
     peers = [{"ep": (ep + d // 4) % 4, "tp": (z + d % 4) % 4} for d in range(1, 16)]
     for peer in peers:
         pl.semaphore_signal(barrier, inc=1, device_id=peer, device_id_type=MESH)
+    for copy in loads:
+        copy.wait()
     pl.semaphore_wait(barrier, 15)
 
     def idx(cc, yy, zz):
@@ -382,8 +388,13 @@
         rcopy(y_buf(n), y_buf(n), ys_s.at[n], ys_r.at[n], sib).wait_recv()
         add(pown.at[n, pl.ds(z, 1), y] if n in ZFIRST else pown.at[n, :, y, :, cols(n)], y_buf(n))
 
+    def out_copy(n):
+        span = pl.ds(starts[n], WIDTHS[n])
+        return pltpu.make_async_copy(out_ref.at[:, span], out_hbm.at[:, span], out_sem.at[n])
+
     def finish(n):
         out_ref[:, starts[n]:starts[n] + WIDTHS[n]] = pown[n, z, y, :, 0:WIDTHS[n]].astype(bf16)
+        out_copy(n).start()
 
     def y_hop(n):
         y_add(n)
@@ -454,6 +465,8 @@
             copy.wait_send()
     for copy in sends:
         copy.wait_send()
+    for n in range(nc):
+        out_copy(n).wait()
     for here, makers in hops:
         @pl.when(here)
         def _():
@@ -471,14 +484,15 @@
         kw = d_model // NK
         f32, bf16 = jnp.float32, jnp.bfloat16
         vm, dma = pltpu.VMEM, pltpu.SemaphoreType.DMA
-        whole = pl.BlockSpec(memory_space=pltpu.VMEM)
         far = pl.BlockSpec(memory_space=pl.ANY)
         return pl.pallas_call(
             moe_kernel,
             out_shape=jax.ShapeDtypeStruct((rows, d_model), bf16),
-            in_specs=[whole, whole, whole, far, far, far],
-            out_specs=whole,
+            in_specs=[far] * 6,
+            out_specs=far,
             scratch_shapes=[
+                vm((rows, d_model), bf16), vm((TOPK, rows), jnp.int32), vm((TOPK, rows), f32), vm((rows, d_model), bf16),
+                dma((3,)), dma((nc,)),
                 vm((NK, 16, rows, kw), bf16),
                 vm((n_exp, 128, 2 * kw), bf16),
                 vm((16, 16, 128), f32),

time: 113 us -> 111 us (0.982)
  Pallas kernels: 111 us -> 109 us
    pallas_call x1, Pallas kernels: 111 us -> 109 us  [local_moe(): pl.pallas_call(moe_kernel, out_shape=jax.ShapeDtypeStruct((rows, d_model)...]
where the time goes in v4:
time: 111 us
  Pallas kernels  109 us (98%)
  local copies, waits for them, and re-layouts  1.67 us (2%)
    pallas_call x1, Pallas kernels, local_moe(): pl.pallas_call(moe_kernel, out_shape=jax.ShapeDtypeStruct((rows, d_model)...  109 us

profile of v4, /device:TPU:0, one launch (start us, length us, event | category | flops | bytes accessed | tf_op | source)
XLA Modules:
  0.0 110.8 jit_solution(16854653854491381175)
XLA Ops:
  0.0 109.1 %shard_map.64 = bf16[64,2048]{1,0:T(8,128)(2,1)} custom-call(bf16[64,2048]{1,0:T(8,128)(2,1)} %x_hbm.1, s32[6,64]{1,0:T(8,128)} %bitcast.6, f32[6,64]{1,0:T(8,128)} %bitcast.7, bf16[16,352,2048]{2,1,0:T(8,128)(2,1)} %bitcast.4, bf16[16,352,2048]{2,1,0:T(8,128)(2,1)} %bitcast.5, bf16[16,352,2048]{2,1,0:T(8,128)(2,1)} %wd.1), custom_call_target="tpu_custom_call" | custom-call | tf_op jit(solution)/shard_map/pallas_call | solution.py:488
  109.1 1.7 %copy.8 = bf16[64,2048]{1,0:T(8,128)(2,1)} copy(bf16[64,2048]{1,0:T(8,128)(2,1)} %shard_map.64) | data formatting | bytes 524288
